TPU v7x, 32 devices: a whole 2x2x4 slice. The times are simulated.
32 devices in a mesh: row: 16 (over z, x, core), col: 2 (over y).
Axes of the slice: x: 2, y: 2, z: 4, core: 2. Of those that a mesh axis runs over, the one named last changes fastest.
Arguments:
- embed_first: bfloat16 [768, 16384], P('col', 'row'), may hold values from -6 to 6
- embed_second: bfloat16 [768, 16384], P('row', 'col'), may hold values from -6 to 6
- corr_grad: float32 [16384, 16384], P('row', 'col'), may hold values from -0.046875 to 0.046875
Outputs:
- grad_first: bfloat16 [768, 16384], P('col', 'row')
- grad_second: bfloat16 [768, 16384], P('row', 'col')
All inputs are finite; a program needn't handle non-finite values.
Results may differ from a plain program's by a relative error of at most 0.0065.
Values may be sent and summed in bfloat16 or wider, within the bound.
A program may use at most 128 MiB of HBM per device.

v0:
```python
import functools

import jax
import jax.numpy as jnp
from jax import lax
from jax.experimental import pallas as pl
from jax.experimental.pallas import tpu as pltpu
from jax.sharding import PartitionSpec as P

FIRST_SHARE = 0.4
TILE = 256
SLOTS = 3


def cuts(fj):
    unit = fj // 256
    short = round(unit * FIRST_SHARE)
    widths = [(True, short), (True, short), (False, unit - short), (False, unit - short)]
    out, at = [], 0
    for kind, w in widths:
        out.append((kind, at, w * 128))
        at += w * 128
    return out


def slots_of(side):
    return 1 if side == 2 else side + 1


def kernel(
    a_side, b_side, cols,
    e1_ref, e2_ref, g_ref, o1_ref, o2_ref,
    e1x, e2x, gb, p2, s2, rb_short, rb_long, acc, t1s, t1r, gt,
    g_sem, e1_send, e1_recv, ag_send, ag_recv, sib_send, sib_recv,
    d2d_send, d2d_recv, rs_send, rs_recv_short, rs_recv_long, t1_send, t1_recv,
):
    chips = a_side * b_side
    block, fj = e2_ref.shape
    rows, fi = e1_ref.shape
    share = chips // cols
    bf16, f32 = jnp.bfloat16, jnp.float32
    pieces = cuts(fj)
    order = [2, 0, 3, 1]
    sides = {"a": a_side, "b": b_side}

    me = lax.axis_index("row")
    my_col = lax.axis_index("col")
    chip, core = me // 2, me % 2
    other = 1 - core
    here = {"a": chip // b_side, "b": chip % b_side}
    sibling = chip * 2 + other

    def at_offset(da, db):
        return chip + da * b_side + db

    def neighbour(axis, sign):
        return (chip + sign * (b_side if axis == "a" else 1)) * 2 + core

    def inside(axis, d):
        where = here[axis] + d
        return jnp.logical_and(where >= 0, where < sides[axis])

    def both_inside(da, db):
        return jnp.logical_and(inside("a", da), inside("b", db))

    def offsets(distance):
        for da in range(a_side - 1, -a_side, -1):
            for db in range(b_side - 1, -b_side, -1):
                if abs(da) + abs(db) == distance:
                    yield da, db

    far = a_side + b_side - 2

    def piece(k):
        return pl.ds(pieces[k][1], pieces[k][2])

    def remote(src, dst, send, recv, **to):
        return pltpu.make_async_remote_copy(
            src_ref=src, dst_ref=dst, send_sem=send, recv_sem=recv,
            device_id=to, device_id_type=pl.DeviceIdType.MESH,
        )

    WAYS = (("a", 1), ("a", -1), ("b", 1), ("b", -1))

    barrier = pltpu.get_barrier_semaphore()
    for axis, sign in WAYS:
        @pl.when(inside(axis, sign))
        def _():
            pl.semaphore_signal(
                barrier, inc=1, device_id={"row": neighbour(axis, sign)}, device_id_type=pl.DeviceIdType.MESH
            )
    pl.semaphore_signal(barrier, inc=1, device_id={"row": sibling}, device_id_type=pl.DeviceIdType.MESH)
    for off in range(1, cols):
        pl.semaphore_signal(
            barrier, inc=1, device_id={"col": (my_col + off) % cols}, device_id_type=pl.DeviceIdType.MESH
        )
    peers = sum(inside(*way).astype(jnp.int32) for way in WAYS)
    pl.semaphore_wait(barrier, peers + cols)

    def block_copy(da, db, k, way):
        src_chip = at_offset(da, db)
        dst = e2x.at[src_chip, core, :, piece(k)]
        src = e2_ref.at[:, piece(k)] if (da, db) == (0, 0) else dst
        return remote(
            src, dst, ag_send.at[src_chip, k, way], ag_recv.at[src_chip, k], row=neighbour(*WAYS[way])
        )

    def sibling_copy(da, db, k):
        src_chip = at_offset(da, db)
        dst = e2x.at[src_chip, core, :, piece(k)]
        src = e2_ref.at[:, piece(k)] if (da, db) == (0, 0) else dst
        return remote(src, dst, sib_send.at[src_chip, k], sib_recv.at[src_chip, k], row=sibling)

    def onward(da, db, k):
        first, second = ("b", "a") if pieces[k][0] else ("a", "b")
        d = {"a": da, "b": db}
        for way, (axis, sign) in enumerate(WAYS):
            if axis == second:
                if d[second] * sign <= 0:
                    yield way
            elif d[second] == 0 and d[first] * sign <= 0:
                yield way

    def send_on(da, db, k):
        for way in onward(da, db, k):
            @pl.when(inside(*WAYS[way]))
            def _():
                block_copy(da, db, k, way).start()

    def gather_round(distance):
        for da, db in offsets(distance):
            @pl.when(both_inside(da, db))
            def _():
                for k in order:
                    block_copy(da, db, k, 0).wait_recv()
                    send_on(da, db, k)
                    sibling_copy(da, db, k).start()

    for k in order:
        send_on(0, 0, k)
    e1_copies = []
    for off in range(1, cols):
        to = (my_col + off) % cols
        e1_copies.append(remote(e1_ref, e1x.at[off - 1], e1_send.at[off - 1], e1_recv.at[off - 1], col=to))
        e1_copies[-1].start()

    def load(n):
        slot = n % SLOTS
        return pltpu.make_async_copy(
            g_ref.at[:, pl.ds(pl.multiple_of(n * TILE, TILE), TILE)], gt.at[slot], g_sem.at[slot]
        )

    tiles = fj // TILE
    for n in range(SLOTS):
        load(n).start()
    for k in order:
        sibling_copy(0, 0, k).start()

    def first_pass(n, carry):
        load(n).wait()
        at = pl.ds(pl.multiple_of(n * TILE, TILE), TILE)
        low = gt[n % SLOTS].astype(bf16)
        gb[:, at] = low

        @pl.when(n + SLOTS < tiles)
        def _():
            load(n + SLOTS).start()

        terms = jnp.dot(e1_ref[...], low, preferred_element_type=f32).astype(bf16)
        p2[pl.ds(my_col * share, share), :, :, at] = terms.reshape(share, 2, block, TILE)
        return carry

    def next_pass(off, wide):
        from_col = (my_col - off + cols) % cols

        def body(n, carry):
            at = pl.ds(pl.multiple_of(n * wide, wide), wide)
            terms = jnp.dot(e1x[off - 1], gb[:, at], preferred_element_type=f32).astype(bf16)
            p2[pl.ds(from_col * share, share), :, :, at] = terms.reshape(share, 2, block, wide)
            return carry

        return body

    def d2d_copy(off, h):
        from_chip = pl.ds((my_col - off + cols) % cols * share, share)
        at = pl.ds(h * (fj // 2), fj // 2)
        return remote(
            p2.at[from_chip, other, :, at], s2.at[from_chip, :, at],
            d2d_send.at[off, h], d2d_recv.at[off, h], row=sibling,
        )

    for h in range(2):
        lax.fori_loop(h * tiles // 2, (h + 1) * tiles // 2, first_pass, 0)
        d2d_copy(0, h).start()
    gather_round(1)
    e2x[chip, core] = e2_ref[...]
    wide = 512
    for off in range(1, cols):
        e1_copies[off - 1].wait_recv()
        for h in range(2):
            lax.fori_loop(h * fj // wide // 2, (h + 1) * fj // wide // 2, next_pass(off, wide), 0)
            d2d_copy(off, h).start()
    for off in range(cols):
        for h in range(2):
            d2d_copy(off, h).wait_recv()

    def sum_slot(k, axis, sign, to):
        short = pieces[k][0]
        first, second = ("a", "b") if short else ("b", "a")
        place = to["a"] if axis == "a" else to["b"]
        slot = 0 if sides[axis] == 2 else (place + 1 if sign > 0 else place)
        if axis == first:
            slot = to[second] * slots_of(sides[first]) + slot
        else:
            slot = sides[second] * slots_of(sides[first]) + slot
        start = pieces[k][1] if short else pieces[k][1] - pieces[2][1]
        buf = rb_short if short else rb_long
        sem = rs_recv_short if short else rs_recv_long
        return buf.at[slot, :, pl.ds(start, pieces[k][2])], sem.at[slot, k % 2]

    def place_of(da, db):
        return {"a": here["a"] + da, "b": here["b"] + db}

    def way_out(da, db, k):
        first, second = ("a", "b") if pieces[k][0] else ("b", "a")
        d = {"a": da, "b": db}
        axis = first if d[first] else second
        return axis, (1 if d[axis] > 0 else -1)

    def sum_copy(da, db, k):
        axis, sign = way_out(da, db, k)
        to_chip = at_offset(da, db)
        dst, sem = sum_slot(k, axis, sign, place_of(da, db))
        return remote(
            p2.at[to_chip, core, :, piece(k)], dst, rs_send.at[to_chip, k], sem, row=neighbour(axis, sign)
        )

    def arrivals(da, db, k):
        first, second = ("a", "b") if pieces[k][0] else ("b", "a")
        d = {"a": da, "b": db}
        out = []
        for sign in (1, -1):
            if d[first] * sign >= 0:
                out.append((first, sign))
        if d[first] == 0:
            for sign in (1, -1):
                if d[second] * sign >= 0:
                    out.append((second, sign))
        return out

    def sum_of(da, db, k):
        at = piece(k)
        to_chip = at_offset(da, db)
        kept = acc.at[:, pl.ds(0, pieces[k][2])]
        kept[...] = p2[to_chip, core, :, at].astype(f32) + s2[to_chip, :, at].astype(f32)
        for axis, sign in arrivals(da, db, k):
            @pl.when(inside(axis, -sign))
            def _():
                buf, sem = sum_slot(k, axis, sign, place_of(da, db))
                remote(buf, buf, rs_send.at[0, k], sem, row=sibling).wait_recv()
                kept[...] += buf[...].astype(f32)
        return kept[...].astype(bf16)

    def sum_round(distance):
        for da, db in offsets(distance):
            @pl.when(both_inside(da, db))
            def _():
                for k in order:
                    p2[at_offset(da, db), core, :, piece(k)] = sum_of(da, db, k)
                    sum_copy(da, db, k).start()

    left_to_sum = list(range(far, 0, -1))
    for distance in range(2, far + 1):
        sum_round(left_to_sum.pop(0))
        gather_round(distance)
    for da in range(1 - a_side, a_side):
        for db in range(1 - b_side, b_side):
            @pl.when(both_inside(da, db))
            def _():
                for k in range(4):
                    sibling_copy(da, db, k).wait_recv()

    def t1_copy(off):
        return remote(
            t1s.at[off - 1], t1r.at[off - 1], t1_send.at[off - 1], t1_recv.at[off - 1],
            col=(my_col + off) % cols,
        )

    def first_terms(of_col, n):
        left_side = e2x[pl.ds(of_col * share, share)].reshape(rows, fj)
        part = gb[pl.ds(pl.multiple_of(n * TILE, TILE), TILE), :]
        return lax.dot_general(left_side, part, (((1,), (1,)), ((), ())), preferred_element_type=f32)

    for off in range(1, cols):
        def send_body(n, carry, off=off):
            at = pl.ds(pl.multiple_of(n * TILE, TILE), TILE)
            t1s[off - 1, :, at] = first_terms((my_col + off) % cols, n).astype(bf16)
            return carry

        lax.fori_loop(0, fi // TILE, send_body, 0)
        t1_copy(off).start()
        if left_to_sum:
            sum_round(left_to_sum.pop(0))

    def keep(n):
        return gt.at[n // 2, pl.ds(pl.multiple_of(n % 2 * rows, rows), rows)]

    def own_body(n, carry):
        keep(n)[...] = first_terms(my_col, n)
        return carry

    lax.fori_loop(0, fi // TILE, own_body, 0)
    while left_to_sum:
        sum_round(left_to_sum.pop(0))

    for off in range(1, cols):
        t1_copy(off).wait_recv()

    def out_body(n, carry):
        at = pl.ds(pl.multiple_of(n * TILE, TILE), TILE)
        total = keep(n)[...]
        for off in range(1, cols):
            total += t1r[off - 1, :, at].astype(f32)
        o1_ref[:, at] = total.astype(bf16)
        return carry

    lax.fori_loop(0, fi // TILE, out_body, 0)

    for k in order:
        o2_ref[:, piece(k)] = sum_of(0, 0, k)

    for da in range(1 - a_side, a_side):
        for db in range(1 - b_side, b_side):
            @pl.when(both_inside(da, db))
            def _():
                for k in range(4):
                    for way in onward(da, db, k):
                        @pl.when(inside(*WAYS[way]))
                        def _():
                            block_copy(da, db, k, way).wait_send()
                    sibling_copy(da, db, k).wait_send()
                    if (da, db) != (0, 0):
                        sum_copy(da, db, k).wait_send()
    for off in range(cols):
        for h in range(2):
            d2d_copy(off, h).wait_send()
    for off in range(1, cols):
        e1_copies[off - 1].wait_send()
        t1_copy(off).wait_send()


def local(rows_size, cols, e1, e2, g):
    chips = rows_size // 2
    a_side = 4
    b_side = chips // a_side
    block, fj = e2.shape
    rows, fi = e1.shape
    bf16 = jnp.bfloat16
    vmem = pl.BlockSpec(memory_space=pltpu.VMEM)
    dma = pltpu.SemaphoreType.DMA
    pieces = cuts(fj)
    short, long = 2 * pieces[0][2], 2 * pieces[2][2]
    short_slots = b_side * slots_of(a_side) + slots_of(b_side)
    long_slots = a_side * slots_of(b_side) + slots_of(a_side)
    return pl.pallas_call(
        functools.partial(kernel, a_side, b_side, cols),
        out_shape=(jax.ShapeDtypeStruct(e1.shape, bf16), jax.ShapeDtypeStruct(e2.shape, bf16)),
        in_specs=[vmem, vmem, pl.BlockSpec(memory_space=pl.ANY)],
        out_specs=(vmem, vmem),
        scratch_shapes=[
            pltpu.VMEM((cols - 1, rows, fi), bf16),
            pltpu.VMEM((chips, 2, block, fj), bf16),
            pltpu.VMEM((fi, fj), bf16),
            pltpu.VMEM((chips, 2, block, fj), bf16),
            pltpu.VMEM((chips, block, fj), bf16),
            pltpu.VMEM((short_slots, block, short), bf16),
            pltpu.VMEM((long_slots, block, long), bf16),
            pltpu.VMEM((block, max(short, long) // 2), jnp.float32),
            pltpu.VMEM((cols - 1, rows, fi), bf16),
            pltpu.VMEM((cols - 1, rows, fi), bf16),
            pltpu.VMEM((SLOTS, fi, TILE), jnp.float32),
            dma((SLOTS,)),
            dma((cols - 1,)), dma((cols - 1,)),
            dma((chips, 4, 4)), dma((chips, 4)),
            dma((chips, 4)), dma((chips, 4)),
            dma((cols, 2)), dma((cols, 2)),
            dma((chips, 4)), dma((short_slots, 2)), dma((long_slots, 2)),
            dma((cols - 1,)), dma((cols - 1,)),
        ],
        compiler_params=pltpu.CompilerParams(
            collective_id=0, has_side_effects=True, vmem_limit_bytes=67043328
        ),
    )(e1, e2, g)


def solution(mesh):
    return jax.shard_map(
        functools.partial(local, mesh.shape["row"], mesh.shape["col"]),
        mesh=mesh,
        in_specs=(P("col", "row"), P("row", "col"), P("row", "col")),
        out_specs=(P("col", "row"), P("row", "col")),
        check_vma=False,
    )
```

profile of v0, /device:TPU:0, one launch (start us, length us, event | category | flops | bytes accessed | tf_op | source)
XLA Modules:
  0.0 121.0 jit_solution(4164108084619500900)
XLA Ops:
  0.6 116.2 %shard_map.50 = (bf16[384,1024]{1,0:T(8,128)(2,1)}, bf16[48,8192]{1,0:T(8,128)(2,1)}) custom-call(bf16[384,1024]{1,0:T(8,128)(2,1)} %e1_ref.1, bf16[48,8192]{1,0:T(8,128)(2,1)} %e2_ref.1, f32[1024,8192]{1,0:T(8,128)} %g_ref.1), custom_call_target="tpu_custom_call" | custom-call | tf_op jit(solution)/shard_map/pallas_call | solution.py:365
  116.8 2.1 %copy.7 = bf16[384,1024]{1,0:T(8,128)(2,1)} copy(bf16[384,1024]{1,0:T(8,128)(2,1)} %get-tuple-element.4) | data formatting | bytes 1572864
  118.9 2.1 %copy.8 = bf16[48,8192]{1,0:T(8,128)(2,1)} copy(bf16[48,8192]{1,0:T(8,128)(2,1)} %get-tuple-element.5) | data formatting | bytes 1572864
where the time goes:
time: 121 us
  Pallas kernels  116 us (96%)
  local copies, waits for them, and re-layouts  4.13 us (3%)
    pallas_call x1, Pallas kernels, local(): pl.pallas_call(functools.partial(kernel, a_side, b_side, cols), out_shape...  116 us
    unnamed x2, local copies, waits for them, and re-layouts  4.13 us

commit v1 on v0

--- a/solution.py
+++ b/solution.py
@@ -7,6 +7,22 @@
 from jax.experimental.pallas import tpu as pltpu
 from jax.sharding import PartitionSpec as P
 
+OWN, OTHER, GATHER, SUMS, FIRST = range(5)
+STEPS = (
+    (OWN, 0, 0, 0), (GATHER, 0, 1, 0), (OWN, 0, 0, 1), (GATHER, 1, 0, 2), (GATHER, 0, 1, 1), (OTHER, 0, 0, 0),
+    (OTHER, 0, 0, 1), (GATHER, 0, 1, 2), (GATHER, 1, 0, 3), (SUMS, 3, 0, 0), (SUMS, 3, 1, 2), (SUMS, 3, 1, 1),
+    (SUMS, 3, 0, 1), (GATHER, 1, 1, 2), (SUMS, 3, 1, 0), (GATHER, 1, 0, 1), (OTHER, 1, 0, 0),
+    (GATHER, 0, 1, 3), (SUMS, 3, 1, 3), (OTHER, 1, 0, 1), (SUMS, 3, 0, 2), (GATHER, 2, 0, 2),
+    (GATHER, 1, 1, 1), (GATHER, 1, 1, 3), (SUMS, 2, 1, 3), (GATHER, 2, 0, 3), (GATHER, 1, 0, 0),
+    (SUMS, 3, 0, 3), (GATHER, 1, 1, 0), (SUMS, 1, 1, 3), (GATHER, 3, 0, 2), (SUMS, 2, 0, 1), (SUMS, 2, 1, 0),
+    (SUMS, 2, 1, 1), (FIRST, 1, 0, 0), (SUMS, 2, 1, 2), (SUMS, 2, 0, 3), (GATHER, 2, 0, 0), (SUMS, 2, 0, 0),
+    (GATHER, 2, 0, 1), (GATHER, 2, 1, 3), (FIRST, 0, 0, 0), (GATHER, 3, 0, 0), (GATHER, 2, 1, 2),
+    (GATHER, 3, 0, 3), (GATHER, 2, 1, 0), (GATHER, 2, 1, 1), (SUMS, 1, 1, 2), (SUMS, 1, 1, 0),
+    (GATHER, 3, 0, 1), (SUMS, 1, 1, 1), (GATHER, 3, 1, 2), (SUMS, 1, 0, 3), (FIRST, 2, 0, 0),
+    (GATHER, 3, 1, 1), (SUMS, 2, 0, 2), (SUMS, 0, 1, 2), (SUMS, 1, 0, 0), (GATHER, 3, 1, 3),
+    (GATHER, 3, 1, 0), (SUMS, 0, 1, 0), (SUMS, 0, 1, 3), (FIRST, 3, 0, 0), (SUMS, 1, 0, 2), (SUMS, 1, 0, 1),
+    (SUMS, 0, 1, 1),
+)
 FIRST_SHARE = 0.4
 TILE = 256
 SLOTS = 3
@@ -29,18 +45,17 @@
 
 def kernel(
     a_side, b_side, cols,
-    e1_ref, e2_ref, g_ref, o1_ref, o2_ref,
-    e1x, e2x, gb, p2, s2, rb_short, rb_long, acc, t1s, t1r, gt,
-    g_sem, e1_send, e1_recv, ag_send, ag_recv, sib_send, sib_recv,
+    e1_hbm, e2_hbm, g_ref, o1_ref, o2_ref,
+    e1_ref, e1x, e2x, gb, p2, s2, rb_short, rb_long, acc, t1s, t1r, gt,
+    in_sem, g_sem, e1_send, e1_recv, ag_send, ag_recv, sib_send, sib_recv,
     d2d_send, d2d_recv, rs_send, rs_recv_short, rs_recv_long, t1_send, t1_recv,
 ):
     chips = a_side * b_side
-    block, fj = e2_ref.shape
-    rows, fi = e1_ref.shape
+    block, fj = e2_hbm.shape
+    rows, fi = e1_hbm.shape
     share = chips // cols
     bf16, f32 = jnp.bfloat16, jnp.float32
     pieces = cuts(fj)
-    order = [2, 0, 3, 1]
     sides = {"a": a_side, "b": b_side}
 
     me = lax.axis_index("row")
@@ -63,14 +78,6 @@
     def both_inside(da, db):
         return jnp.logical_and(inside("a", da), inside("b", db))
 
-    def offsets(distance):
-        for da in range(a_side - 1, -a_side, -1):
-            for db in range(b_side - 1, -b_side, -1):
-                if abs(da) + abs(db) == distance:
-                    yield da, db
-
-    far = a_side + b_side - 2
-
     def piece(k):
         return pl.ds(pieces[k][1], pieces[k][2])
 
@@ -81,6 +88,13 @@
         )
 
     WAYS = (("a", 1), ("a", -1), ("b", 1), ("b", -1))
+
+    inputs = (
+        pltpu.make_async_copy(e2_hbm, e2x.at[chip, core], in_sem.at[0]),
+        pltpu.make_async_copy(e1_hbm, e1_ref, in_sem.at[1]),
+    )
+    for copy in inputs:
+        copy.start()
 
     barrier = pltpu.get_barrier_semaphore()
     for axis, sign in WAYS:
@@ -100,16 +114,14 @@
     def block_copy(da, db, k, way):
         src_chip = at_offset(da, db)
         dst = e2x.at[src_chip, core, :, piece(k)]
-        src = e2_ref.at[:, piece(k)] if (da, db) == (0, 0) else dst
         return remote(
-            src, dst, ag_send.at[src_chip, k, way], ag_recv.at[src_chip, k], row=neighbour(*WAYS[way])
+            dst, dst, ag_send.at[src_chip, k, way], ag_recv.at[src_chip, k], row=neighbour(*WAYS[way])
         )
 
     def sibling_copy(da, db, k):
         src_chip = at_offset(da, db)
         dst = e2x.at[src_chip, core, :, piece(k)]
-        src = e2_ref.at[:, piece(k)] if (da, db) == (0, 0) else dst
-        return remote(src, dst, sib_send.at[src_chip, k], sib_recv.at[src_chip, k], row=sibling)
+        return remote(dst, dst, sib_send.at[src_chip, k], sib_recv.at[src_chip, k], row=sibling)
 
     def onward(da, db, k):
         first, second = ("b", "a") if pieces[k][0] else ("a", "b")
@@ -127,22 +139,60 @@
             def _():
                 block_copy(da, db, k, way).start()
 
-    def gather_round(distance):
-        for da, db in offsets(distance):
-            @pl.when(both_inside(da, db))
-            def _():
-                for k in order:
+    near, late = (0, 1), (2, 3)
+
+    def sides_of(d):
+        return (d, -d) if d else (0,)
+
+    def gather(d, side, k):
+        for db in across if side else (0,):
+            for da in sides_of(d):
+                @pl.when(both_inside(da, db))
+                def _():
                     block_copy(da, db, k, 0).wait_recv()
                     send_on(da, db, k)
                     sibling_copy(da, db, k).start()
 
-    for k in order:
-        send_on(0, 0, k)
-    e1_copies = []
-    for off in range(1, cols):
-        to = (my_col + off) % cols
-        e1_copies.append(remote(e1_ref, e1x.at[off - 1], e1_send.at[off - 1], e1_recv.at[off - 1], col=to))
-        e1_copies[-1].start()
+    across = sorted((db for db in range(1 - b_side, b_side) if db), key=abs)
+
+    inputs[0].wait()
+    for k in late + near:
+        for way in onward(0, 0, k):
+            if WAYS[way][0] == "a":
+                @pl.when(inside(*WAYS[way]))
+                def _():
+                    block_copy(0, 0, k, way).start()
+    for k in near + late:
+        for way in onward(0, 0, k):
+            if WAYS[way][0] == "b":
+                @pl.when(inside(*WAYS[way]))
+                def _():
+                    block_copy(0, 0, k, way).start()
+
+    parts = max(share // b_side, 1)
+    part_chips, part_rows = share // parts, rows // parts
+
+    def part_of(col, q):
+        return jnp.where(col * 2 < cols, q, parts - 1 - q)
+
+    def e1_copy(off, q):
+        at = pl.ds(pl.multiple_of(part_of(my_col, q) * part_rows, part_rows), part_rows)
+        return remote(
+            e1_ref.at[at], e1x.at[off - 1, at], e1_send.at[off - 1, q], e1_recv.at[off - 1, q],
+            col=(my_col + off) % cols,
+        )
+
+    def e1_arrival(off, q):
+        from_col = (my_col - off + cols) % cols
+        at = pl.ds(pl.multiple_of(part_of(from_col, q) * part_rows, part_rows), part_rows)
+        return remote(
+            e1_ref.at[at], e1x.at[off - 1, at], e1_send.at[off - 1, q], e1_recv.at[off - 1, q], col=from_col
+        )
+
+    inputs[1].wait()
+    for q in range(parts):
+        for off in range(1, cols):
+            e1_copy(off, q).start()
 
     def load(n):
         slot = n % SLOTS
@@ -153,7 +203,7 @@
     tiles = fj // TILE
     for n in range(SLOTS):
         load(n).start()
-    for k in order:
+    for k in near + late:
         sibling_copy(0, 0, k).start()
 
     def first_pass(n, carry):
@@ -170,39 +220,49 @@
         p2[pl.ds(my_col * share, share), :, :, at] = terms.reshape(share, 2, block, TILE)
         return carry
 
-    def next_pass(off, wide):
+    def next_pass(off, q, wide):
         from_col = (my_col - off + cols) % cols
+        part = part_of(from_col, q)
+        left = pl.ds(pl.multiple_of(part * part_rows, part_rows), part_rows)
+        to = pl.ds(from_col * share + part * part_chips, part_chips)
 
         def body(n, carry):
             at = pl.ds(pl.multiple_of(n * wide, wide), wide)
-            terms = jnp.dot(e1x[off - 1], gb[:, at], preferred_element_type=f32).astype(bf16)
-            p2[pl.ds(from_col * share, share), :, :, at] = terms.reshape(share, 2, block, wide)
+            terms = jnp.dot(e1x[off - 1, left], gb[:, at], preferred_element_type=f32).astype(bf16)
+            p2[to, :, :, at] = terms.reshape(part_chips, 2, block, wide)
             return carry
 
         return body
 
-    def d2d_copy(off, h):
-        from_chip = pl.ds((my_col - off + cols) % cols * share, share)
+    def d2d_copy(off, q, h):
+        from_col = (my_col - off + cols) % cols
+        if off:
+            chunk = pl.ds(from_col * share + part_of(from_col, q) * part_chips, part_chips)
+        else:
+            chunk = pl.ds(from_col * share, share)
         at = pl.ds(h * (fj // 2), fj // 2)
         return remote(
-            p2.at[from_chip, other, :, at], s2.at[from_chip, :, at],
-            d2d_send.at[off, h], d2d_recv.at[off, h], row=sibling,
-        )
-
-    for h in range(2):
+            p2.at[chunk, other, :, at], s2.at[chunk, :, at],
+            d2d_send.at[off, q, h], d2d_recv.at[off, q, h], row=sibling,
+        )
+
+    wide = 512
+
+    def own_terms(h):
         lax.fori_loop(h * tiles // 2, (h + 1) * tiles // 2, first_pass, 0)
-        d2d_copy(0, h).start()
-    gather_round(1)
-    e2x[chip, core] = e2_ref[...]
-    wide = 512
-    for off in range(1, cols):
-        e1_copies[off - 1].wait_recv()
-        for h in range(2):
-            lax.fori_loop(h * fj // wide // 2, (h + 1) * fj // wide // 2, next_pass(off, wide), 0)
-            d2d_copy(off, h).start()
-    for off in range(cols):
-        for h in range(2):
-            d2d_copy(off, h).wait_recv()
+        d2d_copy(0, 0, h).start()
+
+    def other_terms(q, h):
+        for off in range(1, cols):
+            if h == 0:
+                e1_arrival(off, q).wait_recv()
+            lax.fori_loop(h * fj // wide // 2, (h + 1) * fj // wide // 2, next_pass(off, q, wide), 0)
+            d2d_copy(off, q, h).start()
+
+    def terms_ready(q):
+        for off in range(0 if q == 0 else 1, cols):
+            for h in range(2):
+                d2d_copy(off, q, h).wait_recv()
 
     def sum_slot(k, axis, sign, to):
         short = pieces[k][0]
@@ -261,73 +321,102 @@
                 kept[...] += buf[...].astype(f32)
         return kept[...].astype(bf16)
 
-    def sum_round(distance):
-        for da, db in offsets(distance):
-            @pl.when(both_inside(da, db))
-            def _():
-                for k in order:
+    def send_sums(d, side, k):
+        for db in reversed(across) if side else (0,):
+            for da in sides_of(d):
+                @pl.when(both_inside(da, db))
+                def _():
                     p2[at_offset(da, db), core, :, piece(k)] = sum_of(da, db, k)
                     sum_copy(da, db, k).start()
 
-    left_to_sum = list(range(far, 0, -1))
-    for distance in range(2, far + 1):
-        sum_round(left_to_sum.pop(0))
-        gather_round(distance)
-    for da in range(1 - a_side, a_side):
-        for db in range(1 - b_side, b_side):
-            @pl.when(both_inside(da, db))
+    unit = min(share, b_side)
+    unit_rows = unit * 2 * block
+
+    def t1_copy(off, slot):
+        at = pl.ds(pl.multiple_of(slot * unit_rows, unit_rows), unit_rows)
+        return remote(
+            t1s.at[off - 1, at], t1r.at[off - 1, at], t1_send.at[off - 1, slot], t1_recv.at[off - 1, slot],
+            col=(my_col + off) % cols,
+        )
+
+    def keep(n, slot):
+        return gt.at[n // 2, pl.ds(pl.multiple_of(n % 2 * rows + slot * unit_rows, unit_rows), unit_rows)]
+
+    def first_terms(d):
+        for da in sides_of(d):
+            for db in range(1 - b_side, b_side):
+                @pl.when(both_inside(da, db))
+                def _():
+                    for k in range(4):
+                        sibling_copy(da, db, k).wait_recv()
+
+        def one_side(s, carry):
+            plane = here["a"] + d * (1 - 2 * s)
+
+            @pl.when(jnp.logical_and(plane >= 0, plane < a_side))
             def _():
+                for g in range(b_side // unit):
+                    chunk = plane * (b_side // unit) + g
+                    first_chip = chunk * unit
+                    off = (first_chip // share - my_col + cols) % cols
+                    slot = first_chip % share // unit
+
+                    def body(n, carry):
+                        left_side = e2x[pl.ds(first_chip, unit)].reshape(unit_rows, fj)
+                        part = gb[pl.ds(pl.multiple_of(n * TILE, TILE), TILE), :]
+                        terms = lax.dot_general(
+                            left_side, part, (((1,), (1,)), ((), ())), preferred_element_type=f32
+                        )
+
+                        @pl.when(off == 0)
+                        def _():
+                            keep(n, slot)[...] = terms
+
+                        @pl.when(off != 0)
+                        def _():
+                            at = pl.ds(pl.multiple_of(slot * unit_rows, unit_rows), unit_rows)
+                            to = pl.ds(pl.multiple_of(n * TILE, TILE), TILE)
+                            t1s[off - 1, at, to] = terms.astype(bf16)
+
+                        return carry
+
+                    lax.fori_loop(0, fi // TILE, body, 0)
+
+                    @pl.when(off != 0)
+                    def _():
+                        t1_copy(off, slot).start()
+
+            return carry
+
+        lax.fori_loop(0, 2 if d else 1, one_side, 0)
+
+    ready = 0
+    for kind, d, side, k in STEPS:
+        if kind == OWN:
+            own_terms(k)
+        elif kind == OTHER:
+            for q in (0,) if d == 0 else range(1, parts):
+                other_terms(q, k)
+        elif kind == GATHER:
+            gather(d, side, k)
+        elif kind == SUMS:
+            for q in range(ready, 1 if d == a_side - 1 else parts):
+                terms_ready(q)
+                ready = q + 1
+            send_sums(d, side, k)
+        else:
+            first_terms(d)
+
+    def last_wait(kept):
+        for da in range(1 - a_side, a_side):
+            for db in range(1 - b_side, b_side):
                 for k in range(4):
-                    sibling_copy(da, db, k).wait_recv()
-
-    def t1_copy(off):
-        return remote(
-            t1s.at[off - 1], t1r.at[off - 1], t1_send.at[off - 1], t1_recv.at[off - 1],
-            col=(my_col + off) % cols,
-        )
-
-    def first_terms(of_col, n):
-        left_side = e2x[pl.ds(of_col * share, share)].reshape(rows, fj)
-        part = gb[pl.ds(pl.multiple_of(n * TILE, TILE), TILE), :]
-        return lax.dot_general(left_side, part, (((1,), (1,)), ((), ())), preferred_element_type=f32)
-
-    for off in range(1, cols):
-        def send_body(n, carry, off=off):
-            at = pl.ds(pl.multiple_of(n * TILE, TILE), TILE)
-            t1s[off - 1, :, at] = first_terms((my_col + off) % cols, n).astype(bf16)
-            return carry
-
-        lax.fori_loop(0, fi // TILE, send_body, 0)
-        t1_copy(off).start()
-        if left_to_sum:
-            sum_round(left_to_sum.pop(0))
-
-    def keep(n):
-        return gt.at[n // 2, pl.ds(pl.multiple_of(n % 2 * rows, rows), rows)]
-
-    def own_body(n, carry):
-        keep(n)[...] = first_terms(my_col, n)
-        return carry
-
-    lax.fori_loop(0, fi // TILE, own_body, 0)
-    while left_to_sum:
-        sum_round(left_to_sum.pop(0))
-
-    for off in range(1, cols):
-        t1_copy(off).wait_recv()
-
-    def out_body(n, carry):
-        at = pl.ds(pl.multiple_of(n * TILE, TILE), TILE)
-        total = keep(n)[...]
-        for off in range(1, cols):
-            total += t1r[off - 1, :, at].astype(f32)
-        o1_ref[:, at] = total.astype(bf16)
-        return carry
-
-    lax.fori_loop(0, fi // TILE, out_body, 0)
-
-    for k in order:
-        o2_ref[:, piece(k)] = sum_of(0, 0, k)
+                    axis, _ = way_out(da, db, k)
+                    recent = abs(da) == 1 and axis == "a" or da == 0
+                    if recent == kept and (da, db) != (0, 0):
+                        @pl.when(both_inside(da, db))
+                        def _():
+                            sum_copy(da, db, k).wait_send()
 
     for da in range(1 - a_side, a_side):
         for db in range(1 - b_side, b_side):
@@ -339,14 +428,38 @@
                         def _():
                             block_copy(da, db, k, way).wait_send()
                     sibling_copy(da, db, k).wait_send()
-                    if (da, db) != (0, 0):
-                        sum_copy(da, db, k).wait_send()
     for off in range(cols):
-        for h in range(2):
-            d2d_copy(off, h).wait_send()
+        for q in range(parts if off else 1):
+            for h in range(2):
+                d2d_copy(off, q, h).wait_send()
     for off in range(1, cols):
-        e1_copies[off - 1].wait_send()
-        t1_copy(off).wait_send()
+        for q in range(parts):
+            e1_copy(off, q).wait_send()
+    last_wait(False)
+
+    for off in range(1, cols):
+        for slot in range(share // unit):
+            t1_copy(off, slot).wait_recv()
+
+    def out_body(n, carry):
+        at = pl.ds(pl.multiple_of(n * TILE, TILE), TILE)
+        for slot in range(share // unit):
+            these = pl.ds(slot * unit_rows, unit_rows)
+            total = keep(n, slot)[...]
+            for off in range(1, cols):
+                total += t1r[off - 1, these, at].astype(f32)
+            o1_ref[these, at] = total.astype(bf16)
+        return carry
+
+    lax.fori_loop(0, fi // TILE, out_body, 0)
+
+    for k in late + near:
+        o2_ref[:, piece(k)] = sum_of(0, 0, k)
+
+    last_wait(True)
+    for off in range(1, cols):
+        for slot in range(share // unit):
+            t1_copy(off, slot).wait_send()
 
 
 def local(rows_size, cols, e1, e2, g):
@@ -356,18 +469,21 @@
     block, fj = e2.shape
     rows, fi = e1.shape
     bf16 = jnp.bfloat16
-    vmem = pl.BlockSpec(memory_space=pltpu.VMEM)
+    vmem, hbm = pl.BlockSpec(memory_space=pltpu.VMEM), pl.BlockSpec(memory_space=pl.ANY)
     dma = pltpu.SemaphoreType.DMA
     pieces = cuts(fj)
+    share = chips // cols
+    parts, slots = max(share // b_side, 1), share // min(share, b_side)
     short, long = 2 * pieces[0][2], 2 * pieces[2][2]
     short_slots = b_side * slots_of(a_side) + slots_of(b_side)
     long_slots = a_side * slots_of(b_side) + slots_of(a_side)
     return pl.pallas_call(
         functools.partial(kernel, a_side, b_side, cols),
         out_shape=(jax.ShapeDtypeStruct(e1.shape, bf16), jax.ShapeDtypeStruct(e2.shape, bf16)),
-        in_specs=[vmem, vmem, pl.BlockSpec(memory_space=pl.ANY)],
+        in_specs=[hbm, hbm, hbm],
         out_specs=(vmem, vmem),
         scratch_shapes=[
+            pltpu.VMEM((rows, fi), bf16),
             pltpu.VMEM((cols - 1, rows, fi), bf16),
             pltpu.VMEM((chips, 2, block, fj), bf16),
             pltpu.VMEM((fi, fj), bf16),
@@ -379,13 +495,13 @@
             pltpu.VMEM((cols - 1, rows, fi), bf16),
             pltpu.VMEM((cols - 1, rows, fi), bf16),
             pltpu.VMEM((SLOTS, fi, TILE), jnp.float32),
-            dma((SLOTS,)),
-            dma((cols - 1,)), dma((cols - 1,)),
+            dma((2,)), dma((SLOTS,)),
+            dma((cols - 1, parts)), dma((cols - 1, parts)),
             dma((chips, 4, 4)), dma((chips, 4)),
             dma((chips, 4)), dma((chips, 4)),
-            dma((cols, 2)), dma((cols, 2)),
+            dma((cols, parts, 2)), dma((cols, parts, 2)),
             dma((chips, 4)), dma((short_slots, 2)), dma((long_slots, 2)),
-            dma((cols - 1,)), dma((cols - 1,)),
+            dma((cols - 1, slots)), dma((cols - 1, slots)),
         ],
         compiler_params=pltpu.CompilerParams(
             collective_id=0, has_side_effects=True, vmem_limit_bytes=67043328

time: 121 us -> 110 us (0.909)
  Pallas kernels: 116 us -> 105 us
    pallas_call x1, Pallas kernels: 116 us -> 105 us  [local(): pl.pallas_call(functools.partial(kernel, a_side, b_side, cols), out_shape...]
where the time goes in v1:
time: 110 us; the launch traced here: 109 us
  Pallas kernels  105 us (95%)
  local copies, waits for them, and re-layouts  4.13 us (4%)
    pallas_call x1, Pallas kernels, local(): pl.pallas_call(functools.partial(kernel, a_side, b_side, cols), out_shape...  105 us
    unnamed x2, local copies, waits for them, and re-layouts  4.13 us

profile of v1, /device:TPU:0, one launch (start us, length us, event | category | flops | bytes accessed | tf_op | source)
XLA Modules:
  0.0 109.3 jit_solution(1804386730459599297)
XLA Ops:
  0.6 104.5 %shard_map.50 = (bf16[384,1024]{1,0:T(8,128)(2,1)}, bf16[48,8192]{1,0:T(8,128)(2,1)}) custom-call(bf16[384,1024]{1,0:T(8,128)(2,1)} %e1_hbm.1, bf16[48,8192]{1,0:T(8,128)(2,1)} %e2_hbm.1, f32[1024,8192]{1,0:T(8,128)} %g_ref.1), custom_call_target="tpu_custom_call" | custom-call | tf_op jit(solution)/shard_map/pallas_call | solution.py:480
  105.2 2.1 %copy.7 = bf16[384,1024]{1,0:T(8,128)(2,1)} copy(bf16[384,1024]{1,0:T(8,128)(2,1)} %get-tuple-element.4) | data formatting | bytes 1572864
  107.2 2.1 %copy.8 = bf16[48,8192]{1,0:T(8,128)(2,1)} copy(bf16[48,8192]{1,0:T(8,128)(2,1)} %get-tuple-element.5) | data formatting | bytes 1572864

commit v2 on v1

--- a/solution.py
+++ b/solution.py
@@ -45,9 +45,9 @@
 
 def kernel(
     a_side, b_side, cols,
-    e1_hbm, e2_hbm, g_ref, o1_ref, o2_ref,
-    e1_ref, e1x, e2x, gb, p2, s2, rb_short, rb_long, acc, t1s, t1r, gt,
-    in_sem, g_sem, e1_send, e1_recv, ag_send, ag_recv, sib_send, sib_recv,
+    e1_hbm, e2_hbm, g_ref, o1_hbm, o2_hbm,
+    o1_ref, o2_ref,    e1_ref, e1x, e2x, gb, p2, s2, rb_short, rb_long, acc, t1s, t1r, gt,
+    in_sem, out_sem, g_sem, e1_send, e1_recv, ag_send, ag_recv, sib_send, sib_recv,
     d2d_send, d2d_recv, rs_send, rs_recv_short, rs_recv_long, t1_send, t1_recv,
 ):
     chips = a_side * b_side
@@ -453,13 +453,40 @@
 
     lax.fori_loop(0, fi // TILE, out_body, 0)
 
+    outputs = [pltpu.make_async_copy(o1_ref, o1_hbm, out_sem.at[4])]
+    outputs[0].start()
     for k in late + near:
         o2_ref[:, piece(k)] = sum_of(0, 0, k)
+        outputs.append(pltpu.make_async_copy(o2_ref.at[:, piece(k)], o2_hbm.at[:, piece(k)], out_sem.at[k]))
+        outputs[-1].start()
 
     last_wait(True)
     for off in range(1, cols):
         for slot in range(share // unit):
             t1_copy(off, slot).wait_send()
+    for copy in outputs:
+        copy.wait()
+
+
+def hand_on(cuts_of, *refs):
+    count = len(cuts_of)
+    sources, targets, held = refs[:count], refs[count : 2 * count], refs[2 * count : 3 * count]
+    in_sem, out_sem = refs[3 * count :]
+    reads, writes = [], []
+    for i, pieces_of in enumerate(cuts_of):
+        step = sources[i].shape[0] // pieces_of
+        for n in range(pieces_of):
+            at = pl.ds(n * step, step)
+            sems = in_sem.at[len(reads)], out_sem.at[len(reads)]
+            reads.append(pltpu.make_async_copy(sources[i].at[at], held[i].at[at], sems[0]))
+            writes.append(pltpu.make_async_copy(held[i].at[at], targets[i].at[at], sems[1]))
+    for copy in reads:
+        copy.start()
+    for read, write in zip(reads, writes):
+        read.wait()
+        write.start()
+    for copy in writes:
+        copy.wait()
 
 
 def local(rows_size, cols, e1, e2, g):
@@ -469,7 +496,7 @@
     block, fj = e2.shape
     rows, fi = e1.shape
     bf16 = jnp.bfloat16
-    vmem, hbm = pl.BlockSpec(memory_space=pltpu.VMEM), pl.BlockSpec(memory_space=pl.ANY)
+    hbm = pl.BlockSpec(memory_space=pl.ANY)
     dma = pltpu.SemaphoreType.DMA
     pieces = cuts(fj)
     share = chips // cols
@@ -477,12 +504,15 @@
     short, long = 2 * pieces[0][2], 2 * pieces[2][2]
     short_slots = b_side * slots_of(a_side) + slots_of(b_side)
     long_slots = a_side * slots_of(b_side) + slots_of(a_side)
-    return pl.pallas_call(
+    shapes = jax.ShapeDtypeStruct(e1.shape, bf16), jax.ShapeDtypeStruct(e2.shape, bf16)
+    grads = pl.pallas_call(
         functools.partial(kernel, a_side, b_side, cols),
-        out_shape=(jax.ShapeDtypeStruct(e1.shape, bf16), jax.ShapeDtypeStruct(e2.shape, bf16)),
+        out_shape=shapes,
         in_specs=[hbm, hbm, hbm],
-        out_specs=(vmem, vmem),
+        out_specs=(hbm, hbm),
         scratch_shapes=[
+            pltpu.VMEM((rows, fi), bf16),
+            pltpu.VMEM((block, fj), bf16),
             pltpu.VMEM((rows, fi), bf16),
             pltpu.VMEM((cols - 1, rows, fi), bf16),
             pltpu.VMEM((chips, 2, block, fj), bf16),
@@ -495,7 +525,7 @@
             pltpu.VMEM((cols - 1, rows, fi), bf16),
             pltpu.VMEM((cols - 1, rows, fi), bf16),
             pltpu.VMEM((SLOTS, fi, TILE), jnp.float32),
-            dma((2,)), dma((SLOTS,)),
+            dma((2,)), dma((5,)), dma((SLOTS,)),
             dma((cols - 1, parts)), dma((cols - 1, parts)),
             dma((chips, 4, 4)), dma((chips, 4)),
             dma((chips, 4)), dma((chips, 4)),
@@ -507,6 +537,14 @@
             collective_id=0, has_side_effects=True, vmem_limit_bytes=67043328
         ),
     )(e1, e2, g)
+    cuts_of = 4, block // 16
+    return pl.pallas_call(
+        functools.partial(hand_on, cuts_of),
+        out_shape=shapes,
+        in_specs=[hbm, hbm],
+        out_specs=(hbm, hbm),
+        scratch_shapes=[pltpu.VMEM(each.shape, bf16) for each in shapes] + [dma((sum(cuts_of),))] * 2,
+    )(*grads)
 
 
 def solution(mesh):

time: 110 us -> 108 us (0.982)
  local copies, waits for them, and re-layouts: 4.13 us -> 0 us
    unnamed x2 -> x0, local copies, waits for them, and re-layouts: 4.13 us -> none
    pallas_call x0 -> x1, Pallas kernels: none -> 2.3 us  [local(): pl.pallas_call(functools.partial(hand_on, cuts_of), out_shape=shapes, in_...]
where the time goes in v2:
time: 108 us; the launch traced here: 107 us
  Pallas kernels  106 us (98%)
    pallas_call x1, Pallas kernels, local(): pl.pallas_call(functools.partial(kernel, a_side, b_side, cols), out_shape...  104 us
    pallas_call x1, Pallas kernels, local(): pl.pallas_call(functools.partial(hand_on, cuts_of), out_shape=shapes, in_...  2.3 us

profile of v2, /device:TPU:0, one launch (start us, length us, event | category | flops | bytes accessed | tf_op | source)
XLA Modules:
  0.0 107.1 jit_solution(4753926782019058302)
XLA Ops:
  0.6 104.0 %shard_map.50 = (bf16[384,1024]{1,0:T(8,128)(2,1)}, bf16[48,8192]{1,0:T(8,128)(2,1)}) custom-call(bf16[384,1024]{1,0:T(8,128)(2,1)} %e1_hbm.1, bf16[48,8192]{1,0:T(8,128)(2,1)} %e2_hbm.1, f32[1024,8192]{1,0:T(8,128)} %g_ref.1), custom_call_target="tpu_custom_call" | custom-call | tf_op jit(solution)/shard_map/pallas_call | solution.py:508
  104.7 2.3 %shard_map.51 = (bf16[384,1024]{1,0:T(8,128)(2,1)}, bf16[48,8192]{1,0:T(8,128)(2,1)}) custom-call(bf16[384,1024]{1,0:T(8,128)(2,1)} %get-tuple-element.4.refs_0_, bf16[48,8192]{1,0:T(8,128)(2,1)} %get-tuple-element.5.refs_1_), custom_call_target="tpu_custom_call" | custom-call | tf_op jit(solution)/shard_map/pallas_call | solution.py:541

commit v3 on v1

--- a/solution.py
+++ b/solution.py
@@ -25,7 +25,8 @@
 )
 FIRST_SHARE = 0.4
 TILE = 256
-SLOTS = 3
+SLOTS = 11
+BAND = 256
 
 
 def cuts(fj):
@@ -39,6 +40,10 @@
     return out
 
 
+def chunks_of(fj):
+    return min(16, fj // TILE)
+
+
 def slots_of(side):
     return 1 if side == 2 else side + 1
 
@@ -46,8 +51,8 @@
 def kernel(
     a_side, b_side, cols,
     e1_hbm, e2_hbm, g_ref, o1_ref, o2_ref,
-    e1_ref, e1x, e2x, gb, p2, s2, rb_short, rb_long, acc, t1s, t1r, gt,
-    in_sem, g_sem, e1_send, e1_recv, ag_send, ag_recv, sib_send, sib_recv,
+    e1_ref, e1x, e2x, gb, p2, stage, s2, rb_short, rb_long, gt,
+    free_sem, in_sem, g_sem, e1_send, e1_recv, ag_send, ag_recv, sib_send, sib_recv,
     d2d_send, d2d_recv, rs_send, rs_recv_short, rs_recv_long, t1_send, t1_recv,
 ):
     chips = a_side * b_side
@@ -55,7 +60,7 @@
     rows, fi = e1_hbm.shape
     share = chips // cols
     bf16, f32 = jnp.bfloat16, jnp.float32
-    pieces = cuts(fj)
+    pieces, chunks = cuts(fj), chunks_of(fj)
     sides = {"a": a_side, "b": b_side}
 
     me = lax.axis_index("row")
@@ -89,11 +94,15 @@
 
     WAYS = (("a", 1), ("a", -1), ("b", 1), ("b", -1))
 
-    inputs = (
-        pltpu.make_async_copy(e2_hbm, e2x.at[chip, core], in_sem.at[0]),
-        pltpu.make_async_copy(e1_hbm, e1_ref, in_sem.at[1]),
-    )
-    for copy in inputs:
+    e2_load = pltpu.make_async_copy(e2_hbm, e2x.at[chip, core], in_sem.at[0])
+    e1_loads = [
+        pltpu.make_async_copy(
+            e1_hbm.at[pl.ds((2 * c + half) * block, block)], e1_ref.at[0, c, half], in_sem.at[1 + 2 * c + half]
+        )
+        for c in range(share)
+        for half in range(2)
+    ]
+    for copy in [e2_load] + e1_loads:
         copy.start()
 
     barrier = pltpu.get_barrier_semaphore()
@@ -155,7 +164,7 @@
 
     across = sorted((db for db in range(1 - b_side, b_side) if db), key=abs)
 
-    inputs[0].wait()
+    e2_load.wait()
     for k in late + near:
         for way in onward(0, 0, k):
             if WAYS[way][0] == "a":
@@ -169,35 +178,41 @@
                 def _():
                     block_copy(0, 0, k, way).start()
 
+    unit = min(share, b_side)
+    unit_rows = unit * 2 * block
     parts = max(share // b_side, 1)
-    part_chips, part_rows = share // parts, rows // parts
+    part_chips = share // parts
 
     def part_of(col, q):
         return jnp.where(col * 2 < cols, q, parts - 1 - q)
 
     def e1_copy(off, q):
-        at = pl.ds(pl.multiple_of(part_of(my_col, q) * part_rows, part_rows), part_rows)
+        at = pl.ds(part_of(my_col, q) * part_chips, part_chips)
         return remote(
-            e1_ref.at[at], e1x.at[off - 1, at], e1_send.at[off - 1, q], e1_recv.at[off - 1, q],
+            e1_ref.at[0, at], e1x.at[off - 1, at], e1_send.at[off - 1, q], e1_recv.at[off - 1, q],
             col=(my_col + off) % cols,
         )
 
     def e1_arrival(off, q):
         from_col = (my_col - off + cols) % cols
-        at = pl.ds(pl.multiple_of(part_of(from_col, q) * part_rows, part_rows), part_rows)
+        at = pl.ds(part_of(from_col, q) * part_chips, part_chips)
         return remote(
-            e1_ref.at[at], e1x.at[off - 1, at], e1_send.at[off - 1, q], e1_recv.at[off - 1, q], col=from_col
-        )
-
-    inputs[1].wait()
+            e1_ref.at[0, at], e1x.at[off - 1, at], e1_send.at[off - 1, q], e1_recv.at[off - 1, q], col=from_col
+        )
+
+    for copy in e1_loads:
+        copy.wait()
     for q in range(parts):
         for off in range(1, cols):
             e1_copy(off, q).start()
 
-    def load(n):
-        slot = n % SLOTS
+    bands = fi // BAND
+
+    def load(m):
+        n, at = m // bands, m % bands
         return pltpu.make_async_copy(
-            g_ref.at[:, pl.ds(pl.multiple_of(n * TILE, TILE), TILE)], gt.at[slot], g_sem.at[slot]
+            g_ref.at[pl.ds(pl.multiple_of(at * BAND, BAND), BAND), pl.ds(pl.multiple_of(n * TILE, TILE), TILE)],
+            gt.at[m % SLOTS], g_sem.at[m % SLOTS],
         )
 
     tiles = fj // TILE
@@ -206,63 +221,117 @@
     for k in near + late:
         sibling_copy(0, 0, k).start()
 
-    def first_pass(n, carry):
-        load(n).wait()
-        at = pl.ds(pl.multiple_of(n * TILE, TILE), TILE)
-        low = gt[n % SLOTS].astype(bf16)
-        gb[:, at] = low
-
-        @pl.when(n + SLOTS < tiles)
-        def _():
-            load(n + SLOTS).start()
-
-        terms = jnp.dot(e1_ref[...], low, preferred_element_type=f32).astype(bf16)
-        p2[pl.ds(my_col * share, share), :, :, at] = terms.reshape(share, 2, block, TILE)
-        return carry
-
-    def next_pass(off, q, wide):
+    span = fj // chunks
+    wide = min(2 * TILE, span)
+
+    def ordered(ref, count):
+        mine = ref[:, core].reshape(count * block, fi)
+        return jnp.concatenate([mine, ref[:, other].reshape(count * block, fi)], axis=0)
+
+    def stage_slot(count, c):
+        return c % 2, pl.ds(c // 2 % (share // count) * count, count)
+
+    def put(terms, to, count, c, n, width):
+        at = pl.ds(pl.multiple_of(c * span + n * width, width), width)
+        within = pl.ds(pl.multiple_of(n * width, width), width)
+        half = count * block
+        p2[to, :, at] = terms[:half].reshape(count, block, width)
+        slot, chips_at = stage_slot(count, c)
+        stage[slot, chips_at, :, within] = terms[half:].reshape(count, block, width)
+
+    def group_of(off, q):
+        return 1 + q * (cols - 1) + off - 1 if off else 0
+
+    def d2d_copy(off, q, c):
         from_col = (my_col - off + cols) % cols
-        part = part_of(from_col, q)
-        left = pl.ds(pl.multiple_of(part * part_rows, part_rows), part_rows)
-        to = pl.ds(from_col * share + part * part_chips, part_chips)
-
-        def body(n, carry):
-            at = pl.ds(pl.multiple_of(n * wide, wide), wide)
-            terms = jnp.dot(e1x[off - 1, left], gb[:, at], preferred_element_type=f32).astype(bf16)
-            p2[to, :, :, at] = terms.reshape(part_chips, 2, block, wide)
+        count = part_chips if off else share
+        first = from_col * share + (part_of(from_col, q) * part_chips if off else 0)
+        group = group_of(off, q)
+        slot, chips_at = stage_slot(count, c)
+        return remote(
+            stage.at[slot, chips_at],
+            s2.at[pl.ds(first, count), :, pl.ds(pl.multiple_of(c * span, span), span)],
+            d2d_send.at[group, c], d2d_recv.at[group, c], row=sibling,
+        )
+
+    last_sent = []
+
+    def chunk_loop(off, q, h, fill):
+        half = chunks // 2
+        depth = 2 * parts if off else 2
+        before = list(last_sent)
+
+        def body(i, carry):
+            c = h * half + i
+            for copy in before:
+                @pl.when(i < copy[3])
+                def _():
+                    d2d_copy(copy[0], copy[1], copy[2] + i).wait_send()
+
+            @pl.when(i >= depth)
+            def _():
+                d2d_copy(off, q, c - depth).wait_send()
+
+            fill(c)
+            d2d_copy(off, q, c).start()
             return carry
 
-        return body
-
-    def d2d_copy(off, q, h):
-        from_col = (my_col - off + cols) % cols
-        if off:
-            chunk = pl.ds(from_col * share + part_of(from_col, q) * part_chips, part_chips)
-        else:
-            chunk = pl.ds(from_col * share, share)
-        at = pl.ds(h * (fj // 2), fj // 2)
-        return remote(
-            p2.at[chunk, other, :, at], s2.at[chunk, :, at],
-            d2d_send.at[off, q, h], d2d_recv.at[off, q, h], row=sibling,
-        )
-
-    wide = 512
+        lax.fori_loop(0, half, body, 0)
+        last_sent[:] = [(off, q, h * half + half - depth, depth)]
 
     def own_terms(h):
-        lax.fori_loop(h * tiles // 2, (h + 1) * tiles // 2, first_pass, 0)
-        d2d_copy(0, 0, h).start()
+        to = pl.ds(my_col * share, share)
+
+        def fill(c):
+            def tile(i, carry):
+                n = c * (span // TILE) + i
+                lows = []
+                for r in range(bands):
+                    m = n * bands + r
+                    load(m).wait()
+                    lows.append(gt[m % SLOTS].astype(bf16))
+                    gb[pl.ds(r * BAND, BAND), pl.ds(pl.multiple_of(n * TILE, TILE), TILE)] = lows[-1]
+
+                    @pl.when(m + SLOTS < tiles * bands)
+                    def _():
+                        load(m + SLOTS).start()
+
+                low = jnp.concatenate(lows, axis=0)
+                terms = jnp.dot(ordered(e1_ref.at[0], share), low, preferred_element_type=f32).astype(bf16)
+                put(terms, to, share, c, i, TILE)
+                return carry
+
+            lax.fori_loop(0, span // TILE, tile, 0)
+
+        chunk_loop(0, 0, h, fill)
 
     def other_terms(q, h):
         for off in range(1, cols):
             if h == 0:
                 e1_arrival(off, q).wait_recv()
-            lax.fori_loop(h * fj // wide // 2, (h + 1) * fj // wide // 2, next_pass(off, q, wide), 0)
-            d2d_copy(off, q, h).start()
+            from_col = (my_col - off + cols) % cols
+            first = part_of(from_col, q) * part_chips
+            to = pl.ds(from_col * share + first, part_chips)
+
+            def fill(c):
+                def tile(m, carry):
+                    at = pl.ds(pl.multiple_of(c * span + m * wide, wide), wide)
+                    left = ordered(e1x.at[off - 1, pl.ds(first, part_chips)], part_chips)
+                    terms = jnp.dot(left, gb[:, at], preferred_element_type=f32).astype(bf16)
+                    put(terms, to, part_chips, c, m, wide)
+                    return carry
+
+                lax.fori_loop(0, span // wide, tile, 0)
+
+            chunk_loop(off, q, h, fill)
 
     def terms_ready(q):
         for off in range(0 if q == 0 else 1, cols):
-            for h in range(2):
-                d2d_copy(off, q, h).wait_recv()
+            def body(c, carry):
+                d2d_copy(off, q, c).wait_recv()
+                return carry
+
+            lax.fori_loop(0, chunks, body, 0)
 
     def sum_slot(k, axis, sign, to):
         short = pieces[k][0]
@@ -292,7 +361,7 @@
         to_chip = at_offset(da, db)
         dst, sem = sum_slot(k, axis, sign, place_of(da, db))
         return remote(
-            p2.at[to_chip, core, :, piece(k)], dst, rs_send.at[to_chip, k], sem, row=neighbour(axis, sign)
+            p2.at[to_chip, :, piece(k)], dst, rs_send.at[to_chip, k], sem, row=neighbour(axis, sign)
         )
 
     def arrivals(da, db, k):
@@ -308,39 +377,45 @@
                     out.append((second, sign))
         return out
 
-    def sum_of(da, db, k):
-        at = piece(k)
+    def kept(k, n):
+        width = min(TILE, pieces[k][2] - n * TILE)
+        return gt.at[n, pl.ds(unit_rows, block), pl.ds(0, width)], pl.ds(n * TILE, width)
+
+    def sum_of(da, db, k, out):
+        start, width = pieces[k][1:]
         to_chip = at_offset(da, db)
-        kept = acc.at[:, pl.ds(0, pieces[k][2])]
-        kept[...] = p2[to_chip, core, :, at].astype(f32) + s2[to_chip, :, at].astype(f32)
+        strips = [kept(k, n) for n in range(-(-width // TILE))]
+        for strip, at in strips:
+            whole_at = pl.ds(start + at.start, at.size)
+            strip[...] = p2[to_chip, :, whole_at].astype(f32) + s2[to_chip, :, whole_at].astype(f32)
         for axis, sign in arrivals(da, db, k):
             @pl.when(inside(axis, -sign))
             def _():
                 buf, sem = sum_slot(k, axis, sign, place_of(da, db))
                 remote(buf, buf, rs_send.at[0, k], sem, row=sibling).wait_recv()
-                kept[...] += buf[...].astype(f32)
-        return kept[...].astype(bf16)
+                for strip, at in strips:
+                    strip[...] += buf[:, at].astype(f32)
+        for strip, at in strips:
+            out[:, pl.ds(start + at.start, at.size)] = strip[...].astype(bf16)
 
     def send_sums(d, side, k):
         for db in reversed(across) if side else (0,):
             for da in sides_of(d):
                 @pl.when(both_inside(da, db))
                 def _():
-                    p2[at_offset(da, db), core, :, piece(k)] = sum_of(da, db, k)
+                    sum_of(da, db, k, p2.at[at_offset(da, db)])
                     sum_copy(da, db, k).start()
 
-    unit = min(share, b_side)
-    unit_rows = unit * 2 * block
 
     def t1_copy(off, slot):
-        at = pl.ds(pl.multiple_of(slot * unit_rows, unit_rows), unit_rows)
+        at = pl.ds(slot * unit, unit)
         return remote(
-            t1s.at[off - 1, at], t1r.at[off - 1, at], t1_send.at[off - 1, slot], t1_recv.at[off - 1, slot],
+            e1_ref.at[off - 1, at], e1x.at[off - 1, at], t1_send.at[off - 1, slot], t1_recv.at[off - 1, slot],
             col=(my_col + off) % cols,
         )
 
     def keep(n, slot):
-        return gt.at[n // 2, pl.ds(pl.multiple_of(n % 2 * rows + slot * unit_rows, unit_rows), unit_rows)]
+        return gt.at[n * (share // unit) + slot, pl.ds(0, unit_rows)]
 
     def first_terms(d):
         for da in sides_of(d):
@@ -374,9 +449,9 @@
 
                         @pl.when(off != 0)
                         def _():
-                            at = pl.ds(pl.multiple_of(slot * unit_rows, unit_rows), unit_rows)
                             to = pl.ds(pl.multiple_of(n * TILE, TILE), TILE)
-                            t1s[off - 1, at, to] = terms.astype(bf16)
+                            low = terms.astype(bf16).reshape(unit, 2, block, TILE)
+                            e1_ref[off - 1, pl.ds(slot * unit, unit), :, :, to] = low
 
                         return carry
 
@@ -390,7 +465,16 @@
 
         lax.fori_loop(0, 2 if d else 1, one_side, 0)
 
-    ready = 0
+    def let_terms_in():
+        for off in range(1, cols):
+            for q in range(parts):
+                e1_copy(off, q).wait_send()
+            pl.semaphore_signal(
+                free_sem, inc=1, device_id={"col": (my_col + off) % cols}, device_id_type=pl.DeviceIdType.MESH
+            )
+        pl.semaphore_wait(free_sem, cols - 1)
+
+    ready, open_to_terms = 0, False
     for kind, d, side, k in STEPS:
         if kind == OWN:
             own_terms(k)
@@ -405,6 +489,9 @@
                 ready = q + 1
             send_sums(d, side, k)
         else:
+            if not open_to_terms:
+                let_terms_in()
+                open_to_terms = True
             first_terms(d)
 
     def last_wait(kept):
@@ -428,13 +515,9 @@
                         def _():
                             block_copy(da, db, k, way).wait_send()
                     sibling_copy(da, db, k).wait_send()
-    for off in range(cols):
-        for q in range(parts if off else 1):
-            for h in range(2):
-                d2d_copy(off, q, h).wait_send()
-    for off in range(1, cols):
-        for q in range(parts):
-            e1_copy(off, q).wait_send()
+    for off, q, c, depth in last_sent:
+        for i in range(depth):
+            d2d_copy(off, q, c + i).wait_send()
     last_wait(False)
 
     for off in range(1, cols):
@@ -447,19 +530,30 @@
             these = pl.ds(slot * unit_rows, unit_rows)
             total = keep(n, slot)[...]
             for off in range(1, cols):
-                total += t1r[off - 1, these, at].astype(f32)
+                total += e1x[off - 1, pl.ds(slot * unit, unit), :, :, at].reshape(unit_rows, TILE).astype(f32)
             o1_ref[these, at] = total.astype(bf16)
         return carry
 
     lax.fori_loop(0, fi // TILE, out_body, 0)
 
     for k in late + near:
-        o2_ref[:, piece(k)] = sum_of(0, 0, k)
+        sum_of(0, 0, k, o2_ref)
 
     last_wait(True)
     for off in range(1, cols):
         for slot in range(share // unit):
             t1_copy(off, slot).wait_send()
+
+
+def hand_on(first_ref, second_ref, first_out, second_out, sem):
+    copies = (
+        pltpu.make_async_copy(first_ref, first_out, sem.at[0]),
+        pltpu.make_async_copy(second_ref, second_out, sem.at[1]),
+    )
+    for copy in copies:
+        copy.start()
+    for copy in copies:
+        copy.wait()
 
 
 def local(rows_size, cols, e1, e2, g):
@@ -469,7 +563,7 @@
     block, fj = e2.shape
     rows, fi = e1.shape
     bf16 = jnp.bfloat16
-    vmem, hbm = pl.BlockSpec(memory_space=pltpu.VMEM), pl.BlockSpec(memory_space=pl.ANY)
+    vmem, hbm = pl.BlockSpec(memory_space=pltpu.VMEM), pl.BlockSpec(memory_space=pltpu.HBM)
     dma = pltpu.SemaphoreType.DMA
     pieces = cuts(fj)
     share = chips // cols
@@ -477,36 +571,44 @@
     short, long = 2 * pieces[0][2], 2 * pieces[2][2]
     short_slots = b_side * slots_of(a_side) + slots_of(b_side)
     long_slots = a_side * slots_of(b_side) + slots_of(a_side)
-    return pl.pallas_call(
+    shapes = jax.ShapeDtypeStruct(e1.shape, bf16), jax.ShapeDtypeStruct(e2.shape, bf16)
+    grads = pl.pallas_call(
         functools.partial(kernel, a_side, b_side, cols),
-        out_shape=(jax.ShapeDtypeStruct(e1.shape, bf16), jax.ShapeDtypeStruct(e2.shape, bf16)),
+        out_shape=shapes,
         in_specs=[hbm, hbm, hbm],
         out_specs=(vmem, vmem),
         scratch_shapes=[
-            pltpu.VMEM((rows, fi), bf16),
-            pltpu.VMEM((cols - 1, rows, fi), bf16),
+            pltpu.VMEM((cols - 1, share, 2, block, fi), bf16),
+            pltpu.VMEM((cols - 1, share, 2, block, fi), bf16),
             pltpu.VMEM((chips, 2, block, fj), bf16),
             pltpu.VMEM((fi, fj), bf16),
-            pltpu.VMEM((chips, 2, block, fj), bf16),
+            pltpu.VMEM((chips, block, fj), bf16),
+            pltpu.VMEM((2, share, block, fj // chunks_of(fj)), bf16),
             pltpu.VMEM((chips, block, fj), bf16),
             pltpu.VMEM((short_slots, block, short), bf16),
             pltpu.VMEM((long_slots, block, long), bf16),
-            pltpu.VMEM((block, max(short, long) // 2), jnp.float32),
-            pltpu.VMEM((cols - 1, rows, fi), bf16),
-            pltpu.VMEM((cols - 1, rows, fi), bf16),
-            pltpu.VMEM((SLOTS, fi, TILE), jnp.float32),
-            dma((2,)), dma((SLOTS,)),
+            pltpu.VMEM((SLOTS, BAND, TILE), jnp.float32),
+            pltpu.SemaphoreType.REGULAR,
+            dma((1 + 2 * share,)), dma((SLOTS,)),
             dma((cols - 1, parts)), dma((cols - 1, parts)),
             dma((chips, 4, 4)), dma((chips, 4)),
             dma((chips, 4)), dma((chips, 4)),
-            dma((cols, parts, 2)), dma((cols, parts, 2)),
+            dma((1 + parts * (cols - 1), chunks_of(fj))), dma((1 + parts * (cols - 1), chunks_of(fj))),
             dma((chips, 4)), dma((short_slots, 2)), dma((long_slots, 2)),
             dma((cols - 1, slots)), dma((cols - 1, slots)),
         ],
         compiler_params=pltpu.CompilerParams(
-            collective_id=0, has_side_effects=True, vmem_limit_bytes=67043328
+            collective_id=0, has_side_effects=True, vmem_limit_bytes=54935552
         ),
     )(e1, e2, g)
+    return pl.pallas_call(
+        hand_on,
+        out_shape=shapes,
+        in_specs=[vmem, vmem],
+        out_specs=(hbm, hbm),
+        scratch_shapes=[dma((2,))],
+        compiler_params=pltpu.CompilerParams(vmem_limit_bytes=1 << 22),
+    )(*grads)
 
 
 def solution(mesh):

time: 110 us -> 107 us (0.973)
  local copies, waits for them, and re-layouts: 4.13 us -> 0 us
    unnamed x2 -> x0, local copies, waits for them, and re-layouts: 4.13 us -> none
    pallas_call x0 -> x1, Pallas kernels: none -> 1.16 us  [local(): pl.pallas_call(hand_on, out_shape=shapes, in_specs=[vmem, vmem], out_spec...]
where the time goes in v3:
time: 107 us
  Pallas kernels  106 us (99%)
    pallas_call x1, Pallas kernels, local(): pl.pallas_call(functools.partial(kernel, a_side, b_side, cols), out_shape...  105 us

profile of v3, /device:TPU:0, one launch (start us, length us, event | category | flops | bytes accessed | tf_op | source)
XLA Modules:
  0.0 107.0 jit_solution(16648366535662918755)
XLA Ops:
  0.6 105.0 %shard_map.50 = (bf16[384,1024]{1,0:T(8,128)(2,1)S(1)}, bf16[48,8192]{1,0:T(8,128)(2,1)S(1)}) custom-call(bf16[384,1024]{1,0:T(8,128)(2,1)} %e1_hbm.1, bf16[48,8192]{1,0:T(8,128)(2,1)} %e2_hbm.1, f32[1024,8192]{1,0:T(8,128)} %g_ref.1), custom_call_target="tpu_custom_call" | custom-call | tf_op jit(solution)/shard_map/pallas_call | solution.py:575
  105.6 1.2 %shard_map.51 = (bf16[384,1024]{1,0:T(8,128)(2,1)}, bf16[48,8192]{1,0:T(8,128)(2,1)}) custom-call(bf16[384,1024]{1,0:T(8,128)(2,1)S(1)} %get-tuple-element.4.first_ref, bf16[48,8192]{1,0:T(8,128)(2,1)S(1)} %get-tuple-element.5.second_ref), custom_call_target="tpu_custom_call" | custom-call | tf_op jit(solution)/shard_map/pallas_call | solution.py:604
